TPU v7x, 256 devices: a whole 4x4x8 slice. The times are simulated.
256 devices in a mesh: doc: 16 (over y_lo, z), seq: 16 (over x, y_hi, core).
Axes of the slice: x: 4, y: 4 (y_hi: 2, y_lo: 2; y = y_hi * 2 + y_lo), z: 8, core: 2. Of those that a mesh axis runs over, the one named last changes fastest.
Arguments:
- queries: bfloat16 [131072, 512], P(('doc', 'seq')), parts along dimension 0, may hold values from -5 to 5
- teacher_keys: bfloat16 [131072, 128], P(('doc', 'seq')), parts along dimension 0, may hold values from -5 to 5
- teacher_values: bfloat16 [131072, 128], P(('doc', 'seq')), parts along dimension 0, may hold values from -5 to 5
- beacon_starts: int32 [8192], P(('doc', 'seq')), parts along dimension 0, may hold values from 0 to 511, as said below
Outputs:
- output_gap: bfloat16 [131072, 512], P(('doc', 'seq')), parts along dimension 0
- beacon_key_grad: float32 [8192, 128], P(('doc', 'seq')), parts along dimension 0
- beacon_value_grad: float32 [8192, 128], P(('doc', 'seq')), parts along dimension 0
There are 16 independent parts, one for each index of `doc`. A program takes and returns all parts, laid end to end along the dimension named above; each array names one. Nothing has to cross between parts.
Inputs may be any that keep to these rules, and one draw needn't show every extreme that they name: `beacon_starts`: each aligned block of 32 entries belongs to one shard of 512 tokens: its first entry is 0 and its entries rise strictly.
All inputs are finite; a program needn't handle non-finite values.
Results may differ from a plain program's by a relative error of at most 0.009.
Values may be sent and summed in bfloat16 or wider, within the bound.
No kernel may reach another device: no remote copies, remote signals or barrier semaphores. Data moves between devices by JAX's collectives and lax.ppermute only.
A program may use at most 192 MiB of HBM per device.

v0:
```python
import jax
import jax.numpy as jnp
from jax import lax
from jax.sharding import PartitionSpec as P


def sent_to_all(x, axis):
    length = lax.axis_size(axis)
    return lax.all_to_all(jnp.broadcast_to(x[None], (length, *x.shape)), axis, 0, 0, tiled=True)


def joined_along(pieces, dim):
    pieces = jnp.moveaxis(pieces, 0, dim)
    shape = pieces.shape
    return pieces.reshape(*shape[:dim], shape[dim] * shape[dim + 1], *shape[dim + 2 :])


def gather_directly(x, axis, dim):
    pieces = sent_to_all(x, axis)
    return joined_along(pieces, dim)


def cut_along(x, dim, length):
    shape = x.shape
    pieces = x.reshape(*shape[:dim], length, shape[dim] // length, *shape[dim + 1 :])
    return jnp.moveaxis(pieces, dim, 0)


def summed_on_arrival(x, axis, dim):
    length = lax.axis_size(axis)
    pieces = lax.all_to_all(cut_along(x, dim, length), axis, 0, 0, tiled=True)
    return jnp.sum(pieces.astype(jnp.float32), axis=0)


def fresh_state(row_count, head_size):
    return (
        jnp.full((row_count,), -1e30, jnp.float32),
        jnp.zeros((row_count,), jnp.float32),
        jnp.zeros((row_count, head_size), jnp.float32),
    )


def attend_block(state, query_rows, query_pos, piece, head_size, scaling):
    running, total_weight, accum = state
    key_pos = jnp.arange(piece.shape[0], dtype=jnp.int32)
    scores = (
        jnp.dot(query_rows, piece[:, :head_size].T, preferred_element_type=jnp.float32) * scaling
    )
    scores = jnp.where(key_pos[None, :] <= query_pos[:, None], scores, -jnp.inf)
    highest = jnp.maximum(running, jnp.max(scores, axis=1))
    weights = jnp.exp(scores - highest[:, None])
    total_weight = jnp.sum(weights, axis=1)
    accum = jnp.dot(
        weights.astype(jnp.bfloat16), piece[:, head_size:], preferred_element_type=jnp.float32
    )
    return (highest, total_weight, accum)


def guarded(state, query_rows, query_pos, last_pos, piece, start, head_size, scaling):
    return lax.cond(
        start <= last_pos,
        lambda inner: attend_block(inner, query_rows, query_pos, piece, head_size, scaling),
        lambda inner: inner,
        state,
    )


def body(queries, teacher_keys, teacher_values, beacon_starts):
    tok_here, head_size = teacher_keys.shape
    heads = queries.shape[1] // head_size
    seq_index = lax.axis_index("seq")
    scaling = head_size ** (-0.5)
    beac_here = beacon_starts.shape[0]
    joined = jnp.concatenate([teacher_keys, teacher_values], axis=1)
    positions = jnp.arange(tok_here, dtype=jnp.int32)
    endings = jnp.concatenate([beacon_starts[1:], jnp.full((1,), tok_here, jnp.int32)])
    member = (positions[None, :] >= beacon_starts[:, None]) & (
        positions[None, :] < endings[:, None]
    )
    counts = jnp.sum(member.astype(jnp.float32), axis=1)
    pooled = jnp.dot(member.astype(jnp.bfloat16), joined, preferred_element_type=jnp.float32)
    beacon_rows = (pooled / counts[:, None]).astype(jnp.bfloat16)
    beacons = gather_directly(beacon_rows, "seq", 0)
    first_token = seq_index * tok_here
    last_token = first_token + tok_here - 1
    row_count = tok_here * heads
    query_rows = queries.reshape(row_count, head_size)
    local_pos = jnp.arange(row_count, dtype=jnp.int32) // heads
    initial = fresh_state(row_count, head_size)
    folded = guarded(
        initial,
        query_rows,
        first_token + local_pos,
        last_token,
        lax.all_gather(joined, "seq", axis=0, tiled=True),
        jnp.int32(0),
        head_size,
        scaling,
    )
    teacher = folded[2] / folded[1][:, None]
    beacon_count = beacons.shape[0]
    owners = jnp.arange(beacon_count, dtype=jnp.int32) // beac_here
    keys_all = jnp.concatenate([beacons[:, :head_size], teacher_keys], axis=0)
    values_all = jnp.concatenate([beacons[:, head_size:], teacher_values], axis=0)
    visible = jnp.concatenate(
        [
            jnp.broadcast_to(owners[None, :] < seq_index, (row_count, beacon_count)),
            positions[None, :] <= local_pos[:, None],
        ],
        axis=1,
    )
    student_scores = jnp.where(
        visible,
        jnp.dot(query_rows, keys_all.T, preferred_element_type=jnp.float32) * scaling,
        -jnp.inf,
    )
    student_weights = jnp.exp(student_scores - jnp.max(student_scores, axis=1, keepdims=True))
    student_probs = student_weights / jnp.sum(student_weights, axis=1, keepdims=True)
    probs_low = student_probs.astype(jnp.bfloat16)
    student = jnp.dot(probs_low, values_all, preferred_element_type=jnp.float32)
    output_gap = (student - teacher).astype(jnp.bfloat16)
    prob_grad = jnp.dot(output_gap, values_all.T, preferred_element_type=jnp.float32)
    row_dot = jnp.sum(student_probs * prob_grad, axis=1, keepdims=True)
    score_grad = (student_probs * (prob_grad - row_dot)).astype(jnp.bfloat16)
    grad_keys = (
        jnp.dot(score_grad[:, :beacon_count].T, query_rows, preferred_element_type=jnp.float32)
        * scaling
    )
    grad_values = jnp.dot(
        probs_low[:, :beacon_count].T, output_gap, preferred_element_type=jnp.float32
    )
    grads = summed_on_arrival(
        jnp.concatenate([grad_keys, grad_values], axis=1).astype(jnp.bfloat16), "seq", 0
    )
    return (
        output_gap.reshape(tok_here, heads * head_size),
        grads[:, :head_size],
        grads[:, head_size:],
    )


def solution(mesh):
    in_specs = (
        P(("doc", "seq"), None),
        P(("doc", "seq"), None),
        P(("doc", "seq"), None),
        P(("doc", "seq")),
    )
    out_specs = (P(("doc", "seq"), None), P(("doc", "seq"), None), P(("doc", "seq"), None))
    return jax.shard_map(body, mesh=mesh, in_specs=in_specs, out_specs=out_specs, check_vma=False)
```

profile of v0, /device:TPU:1, one launch (start us, length us, event | category | flops | bytes accessed | tf_op | source)
XLA Modules:
  0.0 178.9 jit_solution(6807393799835753735)
XLA Ops:
  7.2 0.0 all-gather.2.cloned.1.call-start
  7.2 0.9 constant_dynamic-update-slice_fusion.1
  8.1 0.9 constant_dynamic-update-slice_fusion
  9.1 0.0 copy-start.1
  9.1 0.7 copy-done.1
  9.8 0.0 all-gather.2.cloned.1.call-update
  9.8 0.7 slice.27
  10.5 0.1 pad_add_fusion
  10.6 0.8 convert_reduce_fusion.1
  11.5 1.2 fusion.29
  12.6 0.7 broadcast_in_dim.24
  13.4 8.4 %all-to-all-start = ((bf16[16,32,256]{2,1,0:T(8,128)(2,1)}), bf16[16,32,256]{2,1,0:T(8,128)(2,1)S(1)}, u32[]{:S(2)}, u32[]{:S(2)}) async-start(bf16[16,32,256]{2,1,0:T(8,128)(2,1)} %broadcast_in_dim.24), calls=%async_computation | async-start | bytes 524288 | tf_op jit(solution)/shard_map/all_to_all | solution.py:9
  21.8 0.6 iota_compare_fusion.1
  22.4 1.4 reshape.61
  23.8 6.8 %all-to-all-done = bf16[16,32,256]{2,1,0:T(8,128)(2,1)S(1)} async-done(((bf16[16,32,256]{2,1,0:T(8,128)(2,1)}), bf16[16,32,256]{2,1,0:T(8,128)(2,1)S(1)}, u32[]{:S(2)}, u32[]{:S(2)}) %all-to-all-start) | async-done | bytes 262176 | tf_op jit(solution)/shard_map/all_to_all | solution.py:9
  30.7 3.3 %fusion.52 = (f32[2048]{0:T(1024)S(1)}, f32[2048,1024]{0,1:T(8,128)S(1)}) fusion(bf16[2048,128]{1,0:T(8,128)(2,1)S(1)} %reshape.61, bf16[512,128]{1,0:T(8,128)(2,1)} %param.7, bf16[512,128]{1,0:T(8,128)(2,1)S(1)} %get-tuple-element.46, pred[2048,512]{0,1:T(32,128)(4,1)S(1)} %iota_compare_fusion.1, pred[1024]{0:T(1024)(128)(4,1)S(1)} %pad.8.clone), kind=kOutput, calls=%fused_computation.74 | convolution fusion | flops 545781760 | bytes 10232832 | tf_op jit(solution)/shard_map/dot_general | solution.py:114
  34.0 1.2 fusion.13
  35.2 5.4 %fusion.48 = (bf16[2048,1024]{0,1:T(8,128)(2,1)}, f32[2048,1024]{0,1:T(8,128)}) fusion(f32[2048]{0:T(1024)S(1)} %fusion.13, f32[2048,1024]{0,1:T(8,128)S(1)} %get-tuple-element.50, f32[2048]{0:T(1024)S(1)} %get-tuple-element.49), kind=kLoop, calls=%fused_computation.71 | loop fusion | flops 6291456 | bytes 20987904 | tf_op jit(solution)/shard_map/convert_element_type | solution.py:119
  40.5 36.3 %all-gather.2.cloned.1.call-done = bf16[8192,256]{1,0:T(8,128)(2,1)} async-done(((bf16[512,256]{1,0:T(8,128)(2,1)}), bf16[8192,256]{1,0:T(8,128)(2,1)}) %all-gather.2.cloned.1.call-update) | async-done | bytes 4194320 | tf_op jit(solution)/shard_map/all_gather | solution.py:95
  76.8 0.0 copy-start.2
  76.8 73.1 %conditional.1 = (f32[2048]{0:T(1024)S(1)}, f32[2048,128]{1,0:T(8,128)S(1)}) conditional(s32[]{:T(128)} %convert_element_type.30, () %tuple.16, (s32[]{:T(128)}, s32[2048]{0:T(1024)S(1)}, s32[2048]{0:T(1024)S(1)}, bf16[8192,256]{1,0:T(8,128)(2,1)}, bf16[2048,128]{1,0:T(8,128)(2,1)S(1)}) %tuple.17), branch_computations={%region_3.4_spmd, %region_4.0_spmd} | conditional | flops 8824829952 | bytes 207192080 | solution.py:60
  76.8 25.5 %fusion.2 = (f32[2048]{0:T(1024)S(1)}, f32[2048,8192]{1,0:T(8,128)}) fusion(s32[2048]{0:T(1024)S(1)} %fusion.8, bf16[2048,128]{1,0:T(8,128)(2,1)S(1)} %get-tuple-element.32, bf16[8192,256]{1,0:T(8,128)(2,1)} %get-tuple-element.33), kind=kOutput, calls=%fused_computation.5 | convolution fusion | flops 4362074112 | bytes 69746688 | tf_op jit(solution)/shard_map/cond/branch_1_fun/dot_general | solution.py:47
  102.3 25.6 %fusion.3 = f32[2048,128]{1,0:T(8,128)S(1)} fusion(f32[2048,8192]{1,0:T(8,128)} %get-tuple-element.44, f32[2048]{0:T(1024)S(1)} %broadcast_maximum_fusion, s32[2048]{0:T(1024)S(1)} %fusion.8, bf16[8192,256]{1,0:T(8,128)(2,1)} %get-tuple-element.33), kind=kOutput, calls=%fused_computation.6 | convolution fusion | flops 4378853376 | bytes 70270976 | tf_op jit(solution)/shard_map/cond/branch_1_fun/dot_general | solution.py:53
  127.9 22.0 %fusion.1 = f32[2048]{0:T(1024)S(1)} fusion(f32[2048,8192]{1,0:T(8,128)} %get-tuple-element.44, f32[2048]{0:T(1024)S(1)} %broadcast_maximum_fusion, s32[2048]{0:T(1024)S(1)} %fusion.8), kind=kLoop, calls=%fused_computation.4 | loop fusion | flops 83884032 | bytes 67133440 | tf_op jit(solution)/shard_map/cond/branch_1_fun/reduce_sum | solution.py:52
  150.0 0.0 copy-start
  150.0 0.0 slice-start
  150.0 0.0 copy-done.2
  150.0 0.0 slice-start.1
  150.0 3.8 %fusion.15 = bf16[2048,128]{1,0:T(8,128)(2,1)S(1)} fusion(bf16[2048,1024]{0,1:T(8,128)(2,1)} %get-tuple-element.41, f32[2048,128]{1,0:T(8,128)S(1)} %get-tuple-element.39, f32[2048]{0:T(1024)S(1)} %get-tuple-element.40, bf16[512,128]{1,0:T(8,128)(2,1)S(1)} %copy-done.2, bf16[512,128]{1,0:T(8,128)(2,1)S(1)} %get-tuple-element.45), kind=kOutput, calls=%fused_computation.28 | convolution fusion | flops 538181632 | bytes 6037504 | tf_op jit(solution)/shard_map/dot_general | solution.py:120
  153.8 0.0 copy-done
  153.8 0.7 fusion.23
  154.5 0.1 slice-done
  154.7 1.2 slice-done.1
  155.9 1.3 multiply_reduce_fusion
  157.2 0.7 fusion.26
  157.9 0.7 pad_maximum_fusion.1
  158.6 3.9 %all-to-all-start.1 = ((bf16[16,32,256]{2,1,0:T(8,128)(2,1)}), bf16[16,32,256]{2,1,0:T(8,128)(2,1)S(1)}, u32[]{:S(2)}, u32[]{:S(2)}) async-start(bf16[16,32,256]{2,1,0:T(8,128)(2,1)} %pad_maximum_fusion.1), calls=%async_computation.1 | async-start | bytes 524288 | tf_op jit(solution)/shard_map/all_to_all | solution.py:31
  162.5 1.1 reshape.62
  163.7 7.8 %all-to-all-done.1 = bf16[16,32,256]{2,1,0:T(8,128)(2,1)S(1)} async-done(((bf16[16,32,256]{2,1,0:T(8,128)(2,1)}), bf16[16,32,256]{2,1,0:T(8,128)(2,1)S(1)}, u32[]{:S(2)}, u32[]{:S(2)}) %all-to-all-start.1) | async-done | bytes 262176 | tf_op jit(solution)/shard_map/all_to_all | solution.py:31
  171.5 0.6 fusion.51
  (10 shorter events, 0.1 us)
Async XLA Ops:
  7.2 69.7 %all-gather.2.cloned.1.call-start = ((), (), s32[]{:S(2)}) async-start(), calls=%async_computation.2 | async-start | bytes 4456448 | tf_op jit(solution)/shard_map/all_gather | solution.py:95
  9.1 0.7 copy-start.1
  13.4 17.3 %all-to-all-start = ((bf16[16,32,256]{2,1,0:T(8,128)(2,1)}), bf16[16,32,256]{2,1,0:T(8,128)(2,1)S(1)}, u32[]{:S(2)}, u32[]{:S(2)}) async-start(bf16[16,32,256]{2,1,0:T(8,128)(2,1)} %broadcast_in_dim.24), calls=%async_computation | async-start | bytes 524288 | tf_op jit(solution)/shard_map/all_to_all | solution.py:9
  76.8 73.2 %copy-start.2 = (bf16[512,128]{1,0:T(8,128)(2,1)S(1)}, bf16[512,128]{1,0:T(8,128)(2,1)}, u32[]{:S(2)}) copy-start(bf16[512,128]{1,0:T(8,128)(2,1)} %param.8) | copy-start | bytes 393220
  150.0 3.9 %copy-start = (bf16[2048,1024]{0,1:T(8,128)(2,1)S(1)}, bf16[2048,1024]{0,1:T(8,128)(2,1)}, u32[]{:S(2)}) copy-start(bf16[2048,1024]{0,1:T(8,128)(2,1)} %get-tuple-element.41) | copy-start | bytes 12582916
  150.0 4.7 %slice-start = ((s8[8388608]{0:T(1024)(128)(4,1)}), s8[4194304]{0:T(1024)(128)(4,1)S(1)}, s32[]{:S(2)}) async-start(s8[8388608]{0:T(1024)(128)(4,1)} %bitcast.12), calls=%async_computation.3 | async-start | bytes 8388608
  150.0 5.9 %slice-start.1 = ((s8[8388608]{0:T(1024)(128)(4,1)}), s8[4194304]{0:T(1024)(128)(4,1)S(1)}, s32[]{:S(2)}) async-start(s8[8388608]{0:T(1024)(128)(4,1)} %bitcast.12), calls=%async_computation.4 | async-start | bytes 8388608
  158.6 12.8 %all-to-all-start.1 = ((bf16[16,32,256]{2,1,0:T(8,128)(2,1)}), bf16[16,32,256]{2,1,0:T(8,128)(2,1)S(1)}, u32[]{:S(2)}, u32[]{:S(2)}) async-start(bf16[16,32,256]{2,1,0:T(8,128)(2,1)} %pad_maximum_fusion.1), calls=%async_computation.1 | async-start | bytes 524288 | tf_op jit(solution)/shard_map/all_to_all | solution.py:31
Sparse Core Ops, SparseCore 0:
  11.2 65.5 all-gather.1
where the time goes:
time: 179 us
  matrix products  62 us (35%)
  waiting for transfers between devices  50.9 us (28%)
  other arithmetic  30.9 us (17%)
  between operations  14.2 us (8%)
  starting transfers between devices  12.4 us (7%)
  local copies, waits for them, and re-layouts  8.47 us (5%)
    all_gather x1, waiting for transfers between devices, body(): lax.all_gather(joined, 'seq', axis=0, tiled=True)  36.3 us
    dot_general x1, matrix products, attend_block(): jnp.dot(weights.astype(jnp.bfloat16), piece[:, head_size:], preferred_ele...  25.6 us
    dot_general x1, matrix products, attend_block(): jnp.dot(query_rows, piece[:, :head_size].T, preferred_element_type=jnp.fl...  25.5 us
    reduce_sum x1, other arithmetic, attend_block(): total_weight = jnp.sum(weights, axis=1)  22 us
    all_to_all x1, starting transfers between devices, sent_to_all(): lax.all_to_all(jnp.broadcast_to(x[None], (length, *x.shape)), axis, 0, 0,...  8.44 us
    all_to_all x1, waiting for transfers between devices, summed_on_arrival(): pieces = lax.all_to_all(cut_along(x, dim, length), axis, 0, 0, tiled=True)  7.76 us
    all_to_all x1, waiting for transfers between devices, sent_to_all(): lax.all_to_all(jnp.broadcast_to(x[None], (length, *x.shape)), axis, 0, 0,...  6.83 us
    convert_element_type x1, other arithmetic, body(): probs_low = student_probs.astype(jnp.bfloat16)  5.39 us
  transfers between devices with their start and end apart: 3, of which 3 were waited for; matrix products, arithmetic and copies ran while one was open for 9% of the time, Pallas kernels for 0%

commit v1 on v0

--- a/solution.py
+++ b/solution.py
@@ -92,7 +92,9 @@
         query_rows,
         first_token + local_pos,
         last_token,
-        lax.all_gather(joined, "seq", axis=0, tiled=True),
+        jnp.concatenate(
+            lax.all_to_all(jnp.stack([joined] * lax.axis_size("seq")), "seq", 0, 0), axis=0
+        ),
         jnp.int32(0),
         head_size,
         scaling,

time: 179 us -> 186 us (1.039)
  blocking collectives: 0 us -> 17.1 us
  between operations: 14.2 us -> 0.81 us
  starting transfers between devices: 12.4 us -> 17.2 us
  matrix products: 62 us -> 60.1 us
    all_to_all x1, waiting for transfers between devices: 6.83 us -> 43.5 us  [body(): lax.all_to_all(jnp.stack([joined] * lax.axis_size('seq')), 'seq', 0, 0)]
    all_gather x1 -> x0, waiting for transfers between devices: 36.3 us -> none  [body(): lax.all_gather(joined, 'seq', axis=0, tiled=True)]
    all_to_all x0 -> x1, blocking collectives: none -> 17.1 us  [sent_to_all(): lax.all_to_all(jnp.broadcast_to(x[None], (length, *x.shape)), axis, 0, 0,...]
    all_to_all x1, starting transfers between devices: 3.94 us -> 12.5 us  [summed_on_arrival(): pieces = lax.all_to_all(cut_along(x, dim, length), axis, 0, 0, tiled=True)]
    all_to_all x1, starting transfers between devices: 8.44 us -> 4.67 us  [body(): lax.all_to_all(jnp.stack([joined] * lax.axis_size('seq')), 'seq', 0, 0)]
    another operation x0 -> x1, local copies, waits for them, and re-layouts: none -> 2.33 us  [body(): jnp.stack([joined] * lax.axis_size('seq'))]
  transfers between devices with their start and end apart: 3 -> 2, of which waited for: 3 -> 2; matrix products, arithmetic and copies ran while one was open for 9% -> 5% of each run, Pallas kernels for 0% -> 0%
where the time goes in v1:
time: 186 us
  matrix products  60.1 us (32%)
  waiting for transfers between devices  51.2 us (28%)
  other arithmetic  30.9 us (17%)
  starting transfers between devices  17.2 us (9%)
  blocking collectives  17.1 us (9%)
  local copies, waits for them, and re-layouts  8.45 us (5%)
    all_to_all x1, waiting for transfers between devices, body(): lax.all_to_all(jnp.stack([joined] * lax.axis_size('seq')), 'seq', 0, 0)  43.5 us
    dot_general x1, matrix products, attend_block(): jnp.dot(weights.astype(jnp.bfloat16), piece[:, head_size:], preferred_ele...  25.6 us
    dot_general x1, matrix products, attend_block(): jnp.dot(query_rows, piece[:, :head_size].T, preferred_element_type=jnp.fl...  25.5 us
    reduce_sum x1, other arithmetic, attend_block(): total_weight = jnp.sum(weights, axis=1)  22 us
    all_to_all x1, blocking collectives, sent_to_all(): lax.all_to_all(jnp.broadcast_to(x[None], (length, *x.shape)), axis, 0, 0,...  17.1 us
    all_to_all x1, starting transfers between devices, summed_on_arrival(): pieces = lax.all_to_all(cut_along(x, dim, length), axis, 0, 0, tiled=True)  12.5 us
    all_to_all x1, waiting for transfers between devices, summed_on_arrival(): pieces = lax.all_to_all(cut_along(x, dim, length), axis, 0, 0, tiled=True)  7.76 us
    convert_element_type x1, other arithmetic, body(): probs_low = student_probs.astype(jnp.bfloat16)  5.3 us
  transfers between devices with their start and end apart: 2, of which 2 were waited for; matrix products, arithmetic and copies ran while one was open for 5% of the time, Pallas kernels for 0%

profile of v1, /device:TPU:1, one launch (start us, length us, event | category | flops | bytes accessed | tf_op | source)
XLA Modules:
  0.0 185.7 jit_solution(17196813131044252290)
XLA Ops:
  0.6 0.0 copy-start.2
  0.6 0.8 slice.27
  1.4 0.1 pad_add_fusion
  1.5 0.8 convert_reduce_fusion.1
  2.3 0.9 constant_dynamic-update-slice_fusion.1
  3.3 0.9 constant_dynamic-update-slice_fusion
  4.2 0.0 copy-start.3
  4.2 0.9 fusion.29
  5.2 17.1 %all_to_all.15 = bf16[16,32,256]{2,1,0:T(8,128)(2,1)S(1)} all-to-all(bf16[16,32,256]{2,1,0:T(8,128)(2,1)S(1)} %broadcast_in_dim.24), channel_id=1, replica_groups=mesh['doc'=16,'seq'=16] {'seq'}, dimensions={0} | all-to-all | bytes 524288 | tf_op jit(solution)/shard_map/all_to_all | solution.py:9
  22.3 2.3 %stack.2 = bf16[16,512,256]{2,1,0:T(8,128)(2,1)} broadcast(bf16[512,256]{1,0:T(8,128)(2,1)S(1)} %constant_dynamic-update-slice_fusion), dimensions={1,2} | broadcast | bytes 4456448 | tf_op jit(solution)/shard_map/stack | solution.py:96
  24.6 4.7 %all-to-all-start.1 = ((bf16[16,512,256]{2,1,0:T(8,128)(2,1)}), bf16[16,512,256]{2,1,0:T(8,128)(2,1)}, u32[]{:S(2)}, u32[]{:S(2)}) async-start(bf16[16,512,256]{2,1,0:T(8,128)(2,1)} %stack.2), calls=%async_computation.1 | async-start | bytes 8388608 | tf_op jit(solution)/shard_map/all_to_all | solution.py:96
  29.3 0.0 copy-done.2
  29.3 0.3 reshape.67
  29.6 0.6 iota_compare_fusion.1
  30.3 0.0 copy-done.3
  30.3 1.6 fusion.52
  31.9 1.2 fusion.13
  33.1 5.3 %fusion.48 = (bf16[2048,1024]{0,1:T(8,128)(2,1)}, f32[2048,1024]{0,1:T(8,128)}) fusion(f32[2048]{0:T(1024)S(1)} %fusion.13, f32[2048,1024]{0,1:T(8,128)S(1)} %get-tuple-element.51, f32[2048]{0:T(1024)S(1)} %get-tuple-element.50), kind=kLoop, calls=%fused_computation.71 | loop fusion | flops 6291456 | bytes 20987904 | tf_op jit(solution)/shard_map/convert_element_type | solution.py:121
  38.4 43.5 %all-to-all-done.1 = bf16[16,512,256]{2,1,0:T(8,128)(2,1)} async-done(((bf16[16,512,256]{2,1,0:T(8,128)(2,1)}), bf16[16,512,256]{2,1,0:T(8,128)(2,1)}, u32[]{:S(2)}, u32[]{:S(2)}) %all-to-all-start.1) | async-done | bytes 4194336 | tf_op jit(solution)/shard_map/all_to_all | solution.py:96
  81.9 0.0 copy-start.1
  81.9 73.1 %conditional.1 = (f32[2048]{0:T(1024)S(1)}, f32[2048,128]{1,0:T(8,128)S(1)}) conditional(s32[]{:T(128)} %convert_element_type.30, () %tuple.16, (s32[]{:T(128)}, s32[2048]{0:T(1024)S(1)}, s32[2048]{0:T(1024)S(1)}, bf16[16,512,256]{2,1,0:T(8,128)(2,1)}, bf16[2048,128]{1,0:T(8,128)(2,1)S(1)}) %tuple.17), branch_computations={%region_3.4_spmd, %region_4.0_spmd} | conditional | flops 8824829952 | bytes 207192080 | solution.py:60
  81.9 25.5 %fusion.2 = (f32[2048]{0:T(1024)S(1)}, f32[2048,8192]{1,0:T(8,128)}) fusion(s32[2048]{0:T(1024)S(1)} %fusion.8, bf16[2048,128]{1,0:T(8,128)(2,1)S(1)} %get-tuple-element.33, bf16[8192,256]{1,0:T(8,128)(2,1)} %bitcast), kind=kOutput, calls=%fused_computation.5 | convolution fusion | flops 4362074112 | bytes 69746688 | tf_op jit(solution)/shard_map/cond/branch_1_fun/dot_general | solution.py:47
  107.4 25.6 %fusion.3 = f32[2048,128]{1,0:T(8,128)S(1)} fusion(f32[2048,8192]{1,0:T(8,128)} %get-tuple-element.45, f32[2048]{0:T(1024)S(1)} %broadcast_maximum_fusion, s32[2048]{0:T(1024)S(1)} %fusion.8, bf16[8192,256]{1,0:T(8,128)(2,1)} %bitcast), kind=kOutput, calls=%fused_computation.6 | convolution fusion | flops 4378853376 | bytes 70270976 | tf_op jit(solution)/shard_map/cond/branch_1_fun/dot_general | solution.py:53
  133.0 22.0 %fusion.1 = f32[2048]{0:T(1024)S(1)} fusion(f32[2048,8192]{1,0:T(8,128)} %get-tuple-element.45, f32[2048]{0:T(1024)S(1)} %broadcast_maximum_fusion, s32[2048]{0:T(1024)S(1)} %fusion.8), kind=kLoop, calls=%fused_computation.4 | loop fusion | flops 83884032 | bytes 67133440 | tf_op jit(solution)/shard_map/cond/branch_1_fun/reduce_sum | solution.py:52
  155.0 0.0 copy-start
  155.0 0.0 slice-start
  155.0 0.0 copy-done.1
  155.1 0.0 slice-start.1
  155.1 3.8 %fusion.15 = bf16[2048,128]{1,0:T(8,128)(2,1)S(1)} fusion(bf16[2048,1024]{0,1:T(8,128)(2,1)} %get-tuple-element.42, f32[2048,128]{1,0:T(8,128)S(1)} %get-tuple-element.40, f32[2048]{0:T(1024)S(1)} %get-tuple-element.41, bf16[512,128]{1,0:T(8,128)(2,1)S(1)} %copy-done.1, bf16[512,128]{1,0:T(8,128)(2,1)S(1)} %get-tuple-element.46), kind=kOutput, calls=%fused_computation.28 | convolution fusion | flops 538181632 | bytes 6037504 | tf_op jit(solution)/shard_map/dot_general | solution.py:122
  158.9 0.0 copy-done
  158.9 0.7 fusion.23
  159.6 0.2 slice-done
  159.8 1.2 slice-done.1
  161.0 1.3 multiply_reduce_fusion
  162.2 0.7 fusion.26
  162.9 0.7 pad_maximum_fusion.1
  163.7 12.5 %all-to-all-start.2 = ((bf16[16,32,256]{2,1,0:T(8,128)(2,1)}), bf16[16,32,256]{2,1,0:T(8,128)(2,1)S(1)}, u32[]{:S(2)}, u32[]{:S(2)}) async-start(bf16[16,32,256]{2,1,0:T(8,128)(2,1)} %pad_maximum_fusion.1), calls=%async_computation.2 | async-start | bytes 524288 | tf_op jit(solution)/shard_map/all_to_all | solution.py:31
  176.2 1.1 reshape.68
  177.3 7.8 %all-to-all-done.2 = bf16[16,32,256]{2,1,0:T(8,128)(2,1)S(1)} async-done(((bf16[16,32,256]{2,1,0:T(8,128)(2,1)}), bf16[16,32,256]{2,1,0:T(8,128)(2,1)S(1)}, u32[]{:S(2)}, u32[]{:S(2)}) %all-to-all-start.2) | async-done | bytes 262176 | tf_op jit(solution)/shard_map/all_to_all | solution.py:31
  185.1 0.6 fusion.51
  (11 shorter events, 0.1 us)
Async XLA Ops:
  0.6 28.6 %copy-start.2 = (bf16[512,512]{1,0:T(8,128)(2,1)S(1)}, bf16[512,512]{1,0:T(8,128)(2,1)}, u32[]{:S(2)}) copy-start(bf16[512,512]{1,0:T(8,128)(2,1)} %param.6) | copy-start | bytes 1572868
  4.2 26.1 %copy-start.3 = (bf16[512,128]{1,0:T(8,128)(2,1)S(1)}, bf16[512,128]{1,0:T(8,128)(2,1)}, u32[]{:S(2)}) copy-start(bf16[512,128]{1,0:T(8,128)(2,1)} %param.7) | copy-start | bytes 393220
  24.6 57.3 %all-to-all-start.1 = ((bf16[16,512,256]{2,1,0:T(8,128)(2,1)}), bf16[16,512,256]{2,1,0:T(8,128)(2,1)}, u32[]{:S(2)}, u32[]{:S(2)}) async-start(bf16[16,512,256]{2,1,0:T(8,128)(2,1)} %stack.2), calls=%async_computation.1 | async-start | bytes 8388608 | tf_op jit(solution)/shard_map/all_to_all | solution.py:96
  81.9 73.2 %copy-start.1 = (bf16[512,128]{1,0:T(8,128)(2,1)S(1)}, bf16[512,128]{1,0:T(8,128)(2,1)}, u32[]{:S(2)}) copy-start(bf16[512,128]{1,0:T(8,128)(2,1)} %param.8) | copy-start | bytes 393220
  155.0 3.9 %copy-start = (bf16[2048,1024]{0,1:T(8,128)(2,1)S(1)}, bf16[2048,1024]{0,1:T(8,128)(2,1)}, u32[]{:S(2)}) copy-start(bf16[2048,1024]{0,1:T(8,128)(2,1)} %get-tuple-element.42) | copy-start | bytes 12582916
  155.0 4.7 %slice-start = ((s8[8388608]{0:T(1024)(128)(4,1)}), s8[4194304]{0:T(1024)(128)(4,1)S(1)}, s32[]{:S(2)}) async-start(s8[8388608]{0:T(1024)(128)(4,1)} %bitcast.13), calls=%async_computation.3 | async-start | bytes 8388608
  155.1 5.9 %slice-start.1 = ((s8[8388608]{0:T(1024)(128)(4,1)}), s8[4194304]{0:T(1024)(128)(4,1)S(1)}, s32[]{:S(2)}) async-start(s8[8388608]{0:T(1024)(128)(4,1)} %bitcast.13), calls=%async_computation.4 | async-start | bytes 8388608
  163.7 21.4 %all-to-all-start.2 = ((bf16[16,32,256]{2,1,0:T(8,128)(2,1)}), bf16[16,32,256]{2,1,0:T(8,128)(2,1)S(1)}, u32[]{:S(2)}, u32[]{:S(2)}) async-start(bf16[16,32,256]{2,1,0:T(8,128)(2,1)} %pad_maximum_fusion.1), calls=%async_computation.2 | async-start | bytes 524288 | tf_op jit(solution)/shard_map/all_to_all | solution.py:31
